TPU v7x, 32 devices: a whole 2x2x4 slice. The times are simulated.
32 devices in a mesh: groups: 2 (over y), expert: 8 (over z, x), mp: 2 (over core).
Axes of the slice: x: 2, y: 2, z: 4, core: 2. Of those that a mesh axis runs over, the one named last changes fastest.
Arguments:
- tokens: bfloat16 [64, 6144], P(('groups', 'expert', 'mp')), parts along dimension 0, may hold values from -6 to 6
- expert_ids: int32 [64, 2], P(('groups', 'expert', 'mp')), parts along dimension 0, may hold values from 0 to 3, all different within a row; in each aligned block of 2 rows (0 to 1, 2 to 3, ...) at most 2 rows name the same one
- mix_weights: float32 [64, 2], P(('groups', 'expert', 'mp')), parts along dimension 0, may hold values from 0.2 to 1
- w_gate: bfloat16 [6144, 32768], P(None, ('expert', 'mp')), may hold values from -0.078125 to 0.078125
- w_up: bfloat16 [6144, 32768], P(None, ('expert', 'mp')), may hold values from -0.078125 to 0.078125
- w_down: bfloat16 [32768, 6144], P(('expert', 'mp')), may hold values from -0.0625 to 0.0625
Outputs:
- combined: bfloat16 [64, 6144], P(('groups', 'expert', 'mp')), parts along dimension 0
There are 2 independent parts, one for each index of `groups`. A program takes and returns all parts, laid end to end along the dimension named above; an argument that names none is the same for every part. Nothing has to cross between parts.
Inputs may be any that keep to these rules, and one draw needn't show every extreme that they name: `expert_ids`: each row names two different experts. Among the rows of one device no expert is named more than 2 times, and in every draw some device names some expert exactly 2 times.
All inputs are finite; a program needn't handle non-finite values.
Results may differ from a plain program's by a relative error of at most 0.0081.
Values may be sent and summed in bfloat16 or wider, within the bound.
A program may use at most 128 MiB of HBM per device.

v0:
```python
import jax
import jax.numpy as jnp
from jax import lax
from jax.sharding import PartitionSpec as P

EXPERTS = 4
CAP = 2


def feed_forward(arrived_rows, gate_cols, up_cols, down_rows):
    layout = arrived_rows.shape
    flat_rows = arrived_rows.reshape(-1, layout[-1])
    gate_part = jnp.dot(flat_rows, gate_cols, preferred_element_type=jnp.float32)
    up_part = jnp.dot(flat_rows, up_cols, preferred_element_type=jnp.float32)
    hidden = (jax.nn.silu(gate_part) * up_part).astype(jnp.bfloat16)
    partial_value = jnp.dot(hidden, down_rows, preferred_element_type=jnp.float32)
    return partial_value.reshape(layout)


def send_back(partial_value):
    return lax.all_to_all(partial_value, "expert", split_axis=1, concat_axis=0, tiled=True)


def per_device(tokens, expert_ids, mix_weights, w_gate, w_up, w_down):
    shards = lax.axis_size("expert")
    owners = shards // EXPERTS
    tok_rows = tokens.shape[0]
    model_dim = tokens.shape[1]
    expert_range = jnp.arange(EXPERTS, dtype=jnp.int32)
    slot_count = EXPERTS * CAP
    flat_ids = expert_ids.reshape(-1)
    onehot = (flat_ids[:, None] == expert_range[None, :]).astype(jnp.int32)
    earlier = jnp.cumsum(onehot, axis=0) - onehot
    position = flat_ids * CAP + jnp.sum(earlier * onehot, axis=1)
    slot_map = (position[:, None] == jnp.arange(slot_count, dtype=jnp.int32)[None, :]).astype(
        jnp.float32
    )
    slot_map = slot_map.reshape(tok_rows, 2, slot_count)
    token_map = jnp.sum(slot_map, axis=1)
    combine = jnp.sum(slot_map * mix_weights[:, :, None], axis=1)
    compact = jnp.dot(
        token_map.T.astype(jnp.bfloat16), tokens, preferred_element_type=jnp.float32
    ).astype(jnp.bfloat16)
    outgoing = jnp.broadcast_to(
        compact.reshape(EXPERTS, 1, CAP, model_dim), (EXPERTS, owners, CAP, model_dim)
    )
    outgoing = outgoing.reshape(shards, 1, CAP, model_dim)
    paired = lax.all_gather(
        lax.all_to_all(outgoing, "expert", split_axis=0, concat_axis=1, tiled=True),
        "mp",
        axis=0,
        tiled=True,
    )
    partial_value = feed_forward(paired, w_gate, w_up, w_down)
    own_rows = lax.psum_scatter(partial_value, "mp", scatter_dimension=0, tiled=True)
    returned = send_back(own_rows)
    per_expert = jnp.sum(returned.reshape(EXPERTS, owners, CAP, model_dim), axis=1).reshape(
        slot_count, model_dim
    )
    combined = jnp.dot(
        combine, per_expert, precision=lax.Precision.HIGHEST, preferred_element_type=jnp.float32
    )
    return combined.astype(jnp.bfloat16)


def solution(mesh):
    in_specs = (
        P(("groups", "expert", "mp"), None),
        P(("groups", "expert", "mp"), None),
        P(("groups", "expert", "mp"), None),
        P(None, ("expert", "mp")),
        P(None, ("expert", "mp")),
        P(("expert", "mp"), None),
    )
    out_specs = P(("groups", "expert", "mp"), None)
    return jax.shard_map(
        per_device, mesh=mesh, in_specs=in_specs, out_specs=out_specs, check_vma=False
    )
```

profile of v0, /device:TPU:0, one launch (start us, length us, event | category | flops | bytes accessed | tf_op | source)
XLA Modules:
  0.0 93.4 jit_solution(9660064105527126358)
XLA Ops:
  6.5 0.0 copy-start
  6.5 0.0 reduce-scatter.2.cloned.1.call-start
  6.5 0.8 eq.29
  7.3 0.1 fusion.8
  7.4 0.2 select_reduce_fusion.1
  7.6 0.1 reduce_sum.39
  7.7 0.7 multiply_add_fusion
  8.4 0.8 convert_reduce_fusion
  9.1 0.0 copy-done
  9.2 0.2 convolution_convert_fusion
  9.4 0.1 broadcast_in_dim.4
  9.5 0.1 broadcast_in_dim.5
  9.6 15.0 %all_to_all.21 = bf16[8,1,2,6144]{3,2,1,0:T(2,128)(2,1)S(1)} all-to-all(bf16[8,1,2,6144]{3,2,1,0:T(2,128)(2,1)S(1)} %bitcast.12), channel_id=1, replica_groups=mesh['groups'=2,'expert'=8,'mp'=2] {'expert'}, dimensions={0} | all-to-all | bytes 393216 | tf_op jit(solution)/shard_map/all_to_all | solution.py:49
  24.6 2.1 %all-gather = bf16[16,1,2,6144]{3,2,1,0:T(2,128)(2,1)S(1)} all-gather(bf16[8,1,2,6144]{3,2,1,0:T(2,128)(2,1)S(1)} %all_to_all.21), channel_id=2, replica_groups=mesh['groups'=2,'expert'=8,'mp'=2] {'mp'}, dimensions={0}, use_global_device_ids=true | all-gather | bytes 589824 | tf_op jit(solution)/shard_map/all_gather | solution.py:48
  26.7 0.1 reshape.45
  26.8 10.4 %fusion.11 = f32[32,2048]{1,0:T(8,128)S(1)} fusion(bf16[32,6144]{1,0:T(8,128)(2,1)S(1)} %reshape.45, bf16[6144,2048]{1,0:T(8,128)(2,1)} %param.9), kind=kOutput, calls=%fused_computation.20 | convolution fusion | flops 805306368 | bytes 25821184 | tf_op jit(solution)/shard_map/dot_general | solution.py:13
  37.3 19.8 %fusion.1 = f32[32,6144]{1,0:T(8,128)S(1)} fusion(bf16[2048,6144]{1,0:T(8,128)(2,1)} %param.11, bf16[32,6144]{1,0:T(8,128)(2,1)S(1)} %reshape.45, bf16[6144,2048]{1,0:T(8,128)(2,1)} %param.10, f32[32,2048]{1,0:T(8,128)S(1)} %fusion.11), kind=kOutput, calls=%fused_computation.4 | convolution fusion | flops 1611005952 | bytes 51773440 | tf_op jit(solution)/shard_map/dot_general | solution.py:16
  57.1 0.5 reshape.46
  57.6 1.3 %copy.9 = f32[2,8,2,6144]{3,1,2,0:T(8,128)} copy(f32[2,8,2,6144]{3,2,1,0:T(2,128)S(1)} %reshape.46) | data formatting | bytes 1572864 | tf_op jit(solution)/shard_map/reshape | solution.py:17
  58.9 0.0 reduce-scatter.2.cloned.1.call-update
  58.9 6.9 %reduce-scatter.2.cloned.1.call-done = f32[1,8,2,6144]{3,1,2,0:T(8,128)} async-done(((f32[2,8,2,6144]{3,1,2,0:T(8,128)}), f32[1,8,2,6144]{3,1,2,0:T(8,128)}) %reduce-scatter.2.cloned.1.call-update) | async-done | bytes 393232 | tf_op jit(solution)/shard_map/reduce_scatter | solution.py:55
  65.8 1.3 %copy.10 = f32[1,8,2,6144]{3,2,0,1:T(2,128)S(1)} copy(f32[1,8,2,6144]{3,1,2,0:T(8,128)} %reduce-scatter.2.cloned.1.call-done) | data formatting | bytes 786432 | tf_op jit(solution)/shard_map/reduce_scatter | solution.py:55
  67.2 18.1 %all_to_all.22 = f32[1,8,2,6144]{3,2,0,1:T(2,128)S(1)} all-to-all(f32[1,8,2,6144]{3,2,0,1:T(2,128)S(1)} %copy.10), channel_id=1, replica_groups=mesh['groups'=2,'expert'=8,'mp'=2] {'expert'}, dimensions={1} | all-to-all | bytes 786432 | tf_op jit(solution)/shard_map/all_to_all | solution.py:21
  85.2 0.3 reduce_sum.42
  85.5 0.1 reshape.48
  85.7 0.9 convolution_convert_fusion.1
  (1 shorter events, 0.0 us)
Async XLA Ops:
  6.5 2.6 %copy-start = (bf16[2,6144]{1,0:T(2,128)(2,1)S(1)}, bf16[2,6144]{1,0:T(2,128)(2,1)}, u32[]{:S(2)}) copy-start(bf16[2,6144]{1,0:T(2,128)(2,1)} %param.6) | copy-start | bytes 73732
  6.5 59.3 %reduce-scatter.2.cloned.1.call-start = ((), (), s32[]{:S(2)}) async-start(), calls=%async_computation.3 | async-start | bytes 1179648 | tf_op jit(solution)/shard_map/reduce_scatter | solution.py:55
Sparse Core Ops, SparseCore 0:
  59.1 6.7 reduce-scatter.1
where the time goes:
time: 93.8 us; the launch traced here: 93.4 us
  blocking collectives  35.2 us (38%)
  matrix products  31.4 us (33%)
  between operations  13.4 us (14%)
  waiting for transfers between devices  6.93 us (7%)
  local copies, waits for them, and re-layouts  4.43 us (5%)
  other arithmetic  2.04 us (2%)
    dot_general x1, matrix products, feed_forward(): jnp.dot(hidden, down_rows, preferred_element_type=jnp.float32)  19.8 us
    all_to_all x1, blocking collectives, send_back(): lax.all_to_all(partial_value, 'expert', split_axis=1, concat_axis=0, tile...  18.1 us
    all_to_all x1, blocking collectives, per_device(): lax.all_to_all(outgoing, 'expert', split_axis=0, concat_axis=1, tiled=True)  15 us
    dot_general x1, matrix products, feed_forward(): jnp.dot(flat_rows, gate_cols, preferred_element_type=jnp.float32)  10.4 us
    reduce_scatter x1, waiting for transfers between devices, per_device(): lax.psum_scatter(partial_value, 'mp', scatter_dimension=0, tiled=True)  6.92 us
    all_gather x1, blocking collectives, per_device(): lax.all_gather(lax.all_to_all(outgoing, 'expert', split_axis=0, concat_ax...  2.08 us
  transfers between devices with their start and end apart: 1, of which 1 were waited for; matrix products, arithmetic and copies ran while one was open for 0% of the time, Pallas kernels for 0%

commit v1 on v0

--- a/solution.py
+++ b/solution.py
@@ -5,6 +5,13 @@
 
 EXPERTS = 4
 CAP = 2
+
+
+def swap_blocks(value, mesh_axis, split, join):
+    devices = lax.axis_size(mesh_axis)
+    tiles = jnp.stack(jnp.split(value, devices, axis=split), axis=0)
+    tiles = lax.all_to_all(tiles, mesh_axis, split_axis=0, concat_axis=0)
+    return jnp.concatenate(tiles, axis=join)
 
 
 def feed_forward(arrived_rows, gate_cols, up_cols, down_rows):
@@ -18,7 +25,7 @@
 
 
 def send_back(partial_value):
-    return lax.all_to_all(partial_value, "expert", split_axis=1, concat_axis=0, tiled=True)
+    return swap_blocks(partial_value, "expert", 1, 0)
 
 
 def per_device(tokens, expert_ids, mix_weights, w_gate, w_up, w_down):

time: 93.8 us -> 101 us (1.077)
  local copies, waits for them, and re-layouts: 4.43 us -> 11.7 us
    unnamed x2 -> x10, local copies, waits for them, and re-layouts: 0.01 us -> 7.52 us
    reduce_scatter x1 -> x0, local copies, waits for them, and re-layouts: 1.3 us -> none  [per_device(): lax.psum_scatter(partial_value, 'mp', scatter_dimension=0, tiled=True)]
    another operation x0 -> x1, local copies, waits for them, and re-layouts: none -> 1.05 us  [swap_blocks(): tiles = jnp.stack(jnp.split(value, devices, axis=split), axis=0)]
where the time goes in v1:
time: 101 us
  blocking collectives  35.2 us (35%)
  matrix products  31.4 us (31%)
  between operations  13.5 us (13%)
  local copies, waits for them, and re-layouts  11.7 us (12%)
  waiting for transfers between devices  6.93 us (7%)
  other arithmetic  2.05 us (2%)
    dot_general x1, matrix products, feed_forward(): jnp.dot(hidden, down_rows, preferred_element_type=jnp.float32)  19.8 us
    all_to_all x1, blocking collectives, swap_blocks(): tiles = lax.all_to_all(tiles, mesh_axis, split_axis=0, concat_axis=0)  18.1 us
    all_to_all x1, blocking collectives, per_device(): lax.all_to_all(outgoing, 'expert', split_axis=0, concat_axis=1, tiled=True)  15 us
    dot_general x1, matrix products, feed_forward(): jnp.dot(flat_rows, gate_cols, preferred_element_type=jnp.float32)  10.4 us
    unnamed x10, local copies, waits for them, and re-layouts  7.52 us
    reduce_scatter x1, waiting for transfers between devices, per_device(): lax.psum_scatter(partial_value, 'mp', scatter_dimension=0, tiled=True)  6.92 us
    all_gather x1, blocking collectives, per_device(): lax.all_gather(lax.all_to_all(outgoing, 'expert', split_axis=0, concat_ax...  2.08 us
  transfers between devices with their start and end apart: 1, of which 1 were waited for; matrix products, arithmetic and copies ran while one was open for 0% of the time, Pallas kernels for 0%

profile of v1, /device:TPU:0, one launch (start us, length us, event | category | flops | bytes accessed | tf_op | source)
XLA Modules:
  0.0 100.7 jit_solution(10418546287056508496)
XLA Ops:
  6.5 0.0 copy-start
  6.5 0.0 reduce-scatter.2.cloned.1.call-start
  6.5 0.8 eq.29
  7.3 0.1 fusion.16
  7.4 0.2 select_reduce_fusion.1
  7.6 0.1 reduce_sum.39
  7.7 0.7 multiply_add_fusion
  8.4 0.8 convert_reduce_fusion
  9.1 0.0 copy-done
  9.2 0.2 convolution_convert_fusion
  9.4 0.1 broadcast_in_dim.4
  9.5 0.1 broadcast_in_dim.5
  9.6 15.0 %all_to_all.17 = bf16[8,1,2,6144]{3,2,1,0:T(2,128)(2,1)S(1)} all-to-all(bf16[8,1,2,6144]{3,2,1,0:T(2,128)(2,1)S(1)} %bitcast.44), channel_id=1, replica_groups=mesh['groups'=2,'expert'=8,'mp'=2] {'expert'}, dimensions={0} | all-to-all | bytes 393216 | tf_op jit(solution)/shard_map/all_to_all | solution.py:56
  24.6 2.1 %all-gather = bf16[16,1,2,6144]{3,2,1,0:T(2,128)(2,1)S(1)} all-gather(bf16[8,1,2,6144]{3,2,1,0:T(2,128)(2,1)S(1)} %all_to_all.17), channel_id=2, replica_groups=mesh['groups'=2,'expert'=8,'mp'=2] {'mp'}, dimensions={0}, use_global_device_ids=true | all-gather | bytes 589824 | tf_op jit(solution)/shard_map/all_gather | solution.py:55
  26.7 0.1 reshape.38
  26.8 10.4 %fusion.19 = f32[32,2048]{1,0:T(8,128)S(1)} fusion(bf16[32,6144]{1,0:T(8,128)(2,1)S(1)} %reshape.38, bf16[6144,2048]{1,0:T(8,128)(2,1)} %param.9), kind=kOutput, calls=%fused_computation.36 | convolution fusion | flops 805306368 | bytes 25821184 | tf_op jit(solution)/shard_map/dot_general | solution.py:20
  37.3 19.8 %fusion.1 = f32[32,6144]{1,0:T(8,128)S(1)} fusion(bf16[2048,6144]{1,0:T(8,128)(2,1)} %param.11, bf16[32,6144]{1,0:T(8,128)(2,1)S(1)} %reshape.38, bf16[6144,2048]{1,0:T(8,128)(2,1)} %param.10, f32[32,2048]{1,0:T(8,128)S(1)} %fusion.19), kind=kOutput, calls=%fused_computation.4 | convolution fusion | flops 1611005952 | bytes 51773440 | tf_op jit(solution)/shard_map/dot_general | solution.py:23
  57.1 0.5 reshape.39
  57.6 1.3 %copy.8 = f32[2,8,2,6144]{3,1,2,0:T(8,128)} copy(f32[2,8,2,6144]{3,2,1,0:T(2,128)S(1)} %reshape.39) | data formatting | bytes 1572864 | tf_op jit(solution)/shard_map/reshape | solution.py:24
  58.9 0.0 reduce-scatter.2.cloned.1.call-update
  58.9 6.9 %reduce-scatter.2.cloned.1.call-done = f32[1,8,2,6144]{3,1,2,0:T(8,128)} async-done(((f32[2,8,2,6144]{3,1,2,0:T(8,128)}), f32[1,8,2,6144]{3,1,2,0:T(8,128)}) %reduce-scatter.2.cloned.1.call-update) | async-done | bytes 393232 | tf_op jit(solution)/shard_map/reduce_scatter | solution.py:62
  65.8 1.0 %fusion.15 = f32[8,1,1,2,6144]{4,1,3,2,0:T(1,128)S(1)} fusion(f32[1,8,2,6144]{3,1,2,0:T(8,128)} %reduce-scatter.2.cloned.1.call-done), kind=kLoop, calls=%fused_computation.26 | loop fusion | bytes 98304
  66.9 1.0 %fusion.14 = f32[8,1,1,2,6144]{4,1,3,2,0:T(1,128)S(1)} fusion(f32[8,1,1,2,6144]{4,1,3,2,0:T(1,128)S(1)} %fusion.15, f32[1,8,2,6144]{3,1,2,0:T(8,128)} %reduce-scatter.2.cloned.1.call-done), kind=kLoop, calls=%fused_computation.24 | loop fusion | bytes 98304
  67.9 1.0 %fusion.13 = f32[8,1,1,2,6144]{4,1,3,2,0:T(1,128)S(1)} fusion(f32[8,1,1,2,6144]{4,1,3,2,0:T(1,128)S(1)} %fusion.14, f32[1,8,2,6144]{3,1,2,0:T(8,128)} %reduce-scatter.2.cloned.1.call-done), kind=kLoop, calls=%fused_computation.22 | loop fusion | bytes 98304
  69.0 1.0 %fusion.12 = f32[8,1,1,2,6144]{4,1,3,2,0:T(1,128)S(1)} fusion(f32[8,1,1,2,6144]{4,1,3,2,0:T(1,128)S(1)} %fusion.13, f32[1,8,2,6144]{3,1,2,0:T(8,128)} %reduce-scatter.2.cloned.1.call-done), kind=kLoop, calls=%fused_computation.20 | loop fusion | bytes 98304
  70.0 1.0 %fusion.11 = f32[8,1,1,2,6144]{4,1,3,2,0:T(1,128)S(1)} fusion(f32[8,1,1,2,6144]{4,1,3,2,0:T(1,128)S(1)} %fusion.12, f32[1,8,2,6144]{3,1,2,0:T(8,128)} %reduce-scatter.2.cloned.1.call-done), kind=kLoop, calls=%fused_computation.18 | loop fusion | bytes 98304
  71.1 1.0 %fusion.10 = f32[8,1,1,2,6144]{4,1,3,2,0:T(1,128)S(1)} fusion(f32[8,1,1,2,6144]{4,1,3,2,0:T(1,128)S(1)} %fusion.11, f32[1,8,2,6144]{3,1,2,0:T(8,128)} %reduce-scatter.2.cloned.1.call-done), kind=kLoop, calls=%fused_computation.16 | loop fusion | bytes 98304
  72.1 1.0 %fusion.9 = f32[8,1,1,2,6144]{4,1,3,2,0:T(1,128)S(1)} fusion(f32[8,1,1,2,6144]{4,1,3,2,0:T(1,128)S(1)} %fusion.10, f32[1,8,2,6144]{3,1,2,0:T(8,128)} %reduce-scatter.2.cloned.1.call-done), kind=kLoop, calls=%fused_computation.14 | loop fusion | bytes 98304
  73.2 1.0 %fusion.8 = f32[8,1,1,2,6144]{4,1,3,2,0:T(1,128)S(1)} fusion(f32[8,1,1,2,6144]{4,1,3,2,0:T(1,128)S(1)} %fusion.9, f32[1,8,2,6144]{3,1,2,0:T(8,128)} %reduce-scatter.2.cloned.1.call-done), kind=kLoop, calls=%fused_computation.12 | loop fusion | bytes 98304 | tf_op jit(solution)/shard_map/stack | solution.py:12
  74.2 18.1 %all_to_all.18 = f32[8,1,1,2,6144]{4,1,3,2,0:T(1,128)S(1)} all-to-all(f32[8,1,1,2,6144]{4,1,3,2,0:T(1,128)S(1)} %fusion.8), channel_id=1, replica_groups=mesh['groups'=2,'expert'=8,'mp'=2] {'expert'}, dimensions={0} | all-to-all | bytes 786432 | tf_op jit(solution)/shard_map/all_to_all | solution.py:13
  92.3 0.2 copy.9
  92.5 0.3 reduce_sum.42
  92.8 0.1 reshape.40
  92.9 0.9 convolution_convert_fusion.1
  (1 shorter events, 0.0 us)
Async XLA Ops:
  6.5 2.6 %copy-start = (bf16[2,6144]{1,0:T(2,128)(2,1)S(1)}, bf16[2,6144]{1,0:T(2,128)(2,1)}, u32[]{:S(2)}) copy-start(bf16[2,6144]{1,0:T(2,128)(2,1)} %param.6) | copy-start | bytes 73732
  6.5 59.3 %reduce-scatter.2.cloned.1.call-start = ((), (), s32[]{:S(2)}) async-start(), calls=%async_computation.3 | async-start | bytes 1179648 | tf_op jit(solution)/shard_map/reduce_scatter | solution.py:62
Sparse Core Ops, SparseCore 0:
  59.1 6.7 reduce-scatter.1
